TPU v7x, 8 devices: a whole 2x2x1 slice. The times are simulated.
8 devices in a mesh: dp: 2 (over z, y), sp: 4 (over x, core).
Axes of the slice: x: 2, y: 2, z: 1, core: 2. Of those that a mesh axis runs over, the one named last changes fastest.
Arguments:
- pair_rep: float32 [256, 128, 128], P(('dp', 'sp')), parts along dimension 0
- w_qkvg_s: bfloat16 [128, 512], replicated
- w_bias_s: bfloat16 [4, 128], replicated
- w_out_s: bfloat16 [128, 128], replicated
- w_qkvg_e: bfloat16 [128, 512], replicated
- w_bias_e: bfloat16 [4, 128], replicated
- w_out_e: bfloat16 [128, 128], replicated
- w_one: bfloat16 [128, 512], replicated
- w_two: bfloat16 [512, 128], replicated
Outputs:
- output: float32 [256, 128, 128], P(('dp', 'sp')), parts along dimension 0
There are 2 independent parts. A program takes and returns all parts, laid end to end along the dimension named above; an argument that names none is the same for every part.
All inputs are finite; a program needn't handle non-finite values.
Results may differ from a plain program's by a relative error of at most 0.00995982.
Values are sent between devices in bfloat16 or wider.
A program may use at most 1 GiB of HBM per device.

v0:
```python
import functools

import jax
import jax.numpy as jnp
from jax import lax
from jax.experimental import pallas as pl
from jax.experimental.pallas import tpu as pltpu
from jax.sharding import PartitionSpec as P

MESH = pl.DeviceIdType.MESH
EPS = 1e-5
LOG2E = 1.4426950408889634
BF = jnp.bfloat16
F32 = jnp.float32


def dot(a, b):
    return jnp.dot(a, b, preferred_element_type=F32)


def dot_tn(a, b):
    return lax.dot_general(a, b, (((0,), (0,)), ((), ())), preferred_element_type=F32)


def norm_t(xt):
    mean = jnp.sum(xt, axis=0, keepdims=True) * (1.0 / xt.shape[0])
    cen = xt - mean
    var = jnp.sum(cen * cen, axis=0, keepdims=True) * (1.0 / xt.shape[0])
    return (cen * lax.rsqrt(var + EPS)).astype(BF)


def sigmoid(x):
    return 0.5 * jnp.tanh(0.5 * x) + 0.5


def block_diag(qt, pair, heads):
    hd, n = qt.shape
    d = hd // heads
    cols = []
    for h in (2 * pair, 2 * pair + 1):
        parts = []
        if h:
            parts.append(jnp.zeros((h * d, n), BF))
        parts.append(qt[h * d:(h + 1) * d])
        if h < heads - 1:
            parts.append(jnp.zeros(((heads - 1 - h) * d, n), BF))
        cols.append(jnp.concatenate(parts, axis=0))
    return jnp.concatenate(cols, axis=1)


def stage_scores(kn, qv, s, p, heads):
    c, n = kn.shape[1:]
    for r in range(2):
        keys = kn[2 * p + r]
        qt = qv[p, :c, r * n:(r + 1) * n]
        for pair in range(heads // 2):
            s[r, :, 2 * pair * n:(2 * pair + 2) * n] = dot(keys, block_diag(qt, pair, heads))


def stage_mix(s, biast, qv, g, og, p, heads):
    n = s.shape[1]
    c = qv.shape[1] // 2
    d = c // heads
    scale = LOG2E * d ** -0.5
    for r in range(2):
        for pair in range(heads // 2):
            probs = []
            for h in (2 * pair, 2 * pair + 1):
                t = s[r, :, h * n:(h + 1) * n] * scale + biast[:, h * n:(h + 1) * n]
                e = jnp.exp2(t - jnp.max(t, axis=0, keepdims=True))
                probs.append((e * (1.0 / jnp.sum(e, axis=0, keepdims=True))).astype(BF))
            rows = slice(c + 2 * pair * d, c + (2 * pair + 2) * d)
            o = dot(qv[p, rows, r * n:(r + 1) * n], jnp.concatenate(probs, axis=1))
            for i in range(2):
                h = 2 * pair + i
                out = o[i * d:(i + 1) * d, i * n:(i + 1) * n] * g[p, h * d:(h + 1) * d, r * n:(r + 1) * n]
                og[p, h * d:(h + 1) * d, r * n:(r + 1) * n] = out.astype(BF)


def norm_blocks(src, ut, b0, count):
    for r in range(count):
        ut[b0 + r] = norm_t(src[b0 + r])


def head_rows(wb):
    heads, c = wb.shape
    rep = jnp.broadcast_to(wb.astype(F32)[:, None, :], (heads, 8, c)).reshape(heads * 8, c)
    row = lax.broadcasted_iota(jnp.int32, rep.shape, 0) % 8
    return jnp.concatenate([jnp.where(row == j, rep, 0.0) for j in range(8)], axis=1).astype(BF)


def bias_rows(w8, ub, dst, swap=None):
    heads, rows, n = dst.shape
    c = ub.shape[1]
    half = n // 2
    for i in range(rows // 16):
        r0, r1 = [dot(w8, ub[s * rows // 2 + 8 * i:s * rows // 2 + 8 * i + 8].reshape(8 * c, n)) for s in range(2)]
        parts = []
        for lane in (0, half):
            own, oth = r0[:, lane:lane + half], r1[:, lane:lane + half]
            row = jnp.concatenate([own, oth], axis=1)
            if swap is not None:
                row = jnp.where(swap, jnp.concatenate([oth, own], axis=1), row)
            parts.append(row.reshape(heads, 8, n))
        first, second = parts
        dst[:, 16 * i:16 * i + 16] = jnp.concatenate([first[:, :4], second[:, :4], first[:, 4:], second[:, 4:]], axis=1).astype(BF)


def low_half(shape):
    return lax.broadcasted_iota(jnp.int32, shape, 1) < shape[1] // 2


def pair_project(wt, ub, qb, kt_ref, vst, g, p, npair, heads):
    own, oth = ub[p], ub[npair + p]
    c, n = own.shape
    d, half = c // heads, n // 2
    u = jnp.concatenate([own, oth], axis=1)
    q = dot(wt[0:c], u).astype(BF)
    qb[p] = q[:, :n]
    qb[npair + p] = q[:, n:]
    u_row = jnp.concatenate([own[:, :half], oth[:, :half], own[:, half:], oth[:, half:]], axis=1)
    k = dot(wt[c:2 * c], u_row).astype(BF)
    v = dot(wt[2 * c:3 * c], u_row).astype(BF)
    for h in range(heads):
        for i in range(2):
            rows = pl.ds((h % 2) * 2 * d + i * d, d)
            kt_ref[h // 2, rows] = k[h * d:(h + 1) * d, i * n:(i + 1) * n]
            vst[p, h // 2, rows] = v[h * d:(h + 1) * d, i * n:(i + 1) * n]
    gate = sigmoid(dot(wt[3 * c:], u))
    g[p] = gate[:, :n]
    g[npair + p] = gate[:, n:]


def block_scores(kn, qb, s, slot, b, p, heads):
    c, n = qb.shape[1:]
    d = c // heads
    low = low_half((d, n))
    zero = jnp.zeros((d, n), BF)
    for pair in range(heads // 2):
        rows = []
        for i in range(2):
            q = qb[b, (2 * pair + i) * d:(2 * pair + i + 1) * d]
            for part in (jnp.where(low, q, zero), jnp.where(low, zero, q)):
                rows.append(jnp.concatenate([part, zero] if i == 0 else [zero, part], axis=1))
        s[slot, :, 2 * pair * n:(2 * pair + 2) * n] = dot(kn[p, pair], jnp.concatenate(rows, axis=0))


def softmax_t(t):
    e = jnp.exp2(t - jnp.max(t, axis=0, keepdims=True))
    return (e * (1.0 / jnp.sum(e, axis=0, keepdims=True))).astype(BF)


def block_mix(s, slot, biast, side, vst, g, og, b, p, heads):
    c, n = og.shape[1:]
    d = c // heads
    low = low_half((d, n))
    for h in range(heads):
        t = s[slot, :, h * n:(h + 1) * n] * (LOG2E * d ** -0.5) + biast[side, :, h * n:(h + 1) * n]
        o = dot(vst[p, h // 2, (h % 2) * 2 * d:(h % 2 + 1) * 2 * d], softmax_t(t))
        og[b, h * d:(h + 1) * d] = (jnp.where(low, o[:d], o[d:]) * g[b, h * d:(h + 1) * d]).astype(BF)


def project(wt, u, n, qv_ref, kt_ref, g_ref, p):
    c = u.shape[0]
    qv_ref[p, :c] = dot(wt[0:c], u).astype(BF)
    kt_ref[...] = dot(wt[c:2 * c], u).astype(BF)
    qv_ref[p, c:] = dot(wt[2 * c:3 * c], u).astype(BF)
    g_ref[p] = sigmoid(dot(wt[3 * c:], u))


def turn_keys(kt_ref, kn_ref, p):
    n = kn_ref.shape[1]
    kn_ref[2 * p] = kt_ref[:, :n].T
    kn_ref[2 * p + 1] = kt_ref[:, n:].T


def kernel(z_hbm, wqs_h, wbs_h, wos_h, wqe_h, wbe_h, woe_h, w1_h, w2_h, y,
           zs, z1, ub, qb, vst, knp, gb, ogb, bsend, ball, biasp, hsend,
           hcol, qv, kn, g, og, besend, beall, biast, dsend, drecv, s, eb, u2, kt, ktp,
           wqs, wbs, wos, wqe, wbe, woe, w1, w2, wqst, wqet, woet, w1t, w2t, wbs8, wbe8,
           zsem, wsem, bs_s, bs_r, h_s, h_r, o_s, o_r, be_s, be_r, d_s, d_r):
    rows, n, c = y.shape
    npair = rows // 2
    half = n // 2
    heads = wbs.shape[0]
    dp, sp = lax.axis_index("dp"), lax.axis_index("sp")
    x, core = sp // 2, sp % 2
    peers = [2 * (1 - x) + core, 2 * (1 - x) + 1 - core, 2 * x + 1 - core]
    mine = pl.multiple_of(sp * rows, rows)

    def zcopy(ci, i):
        q, side = ci // 2, ci % 2
        return pltpu.make_async_copy(z_hbm.at[q, i, :, pl.ds(pl.multiple_of((x + side) % 2 * half, half), half)],
                                     zs.at[pl.ds(side * npair + 4 * q, 4), pl.ds(i * half, half)], zsem.at[ci, i])

    def wcopy(i):
        src = (wbs_h, wqs_h, wqe_h, woe_h, w1_h, w2_h, wbe_h, wos_h)[i]
        return pltpu.make_async_copy(src, (wbs, wqs, wqe, woe, w1, w2, wbe, wos)[i], wsem.at[i])

    for ci in range(8):
        zcopy(ci, 0).start()
        zcopy(ci, 1).start()
        if ci == 1:
            wcopy(0).start()
            wcopy(1).start()
    for i in range(2, 8):
        wcopy(i).start()
    bar = pltpu.get_barrier_semaphore()
    for t in peers:
        pl.semaphore_signal(bar, inc=1, device_id=(dp, t), device_id_type=MESH)

    def remote(src, dst, ssem, rsem, t):
        return pltpu.make_async_remote_copy(src, dst, ssem, rsem, device_id=(dp, t), device_id_type=MESH)

    def chunk_base(ci):
        return ci % 2 * npair + ci // 2 * 4

    def ln_step(ci, _):
        norm_blocks(y, ub, chunk_base(jnp.maximum(ci - 1, 0)), 4)
        zcopy(ci, 0).wait()
        zcopy(ci, 1).wait()
        b0 = chunk_base(ci)
        for r in range(4):
            y[b0 + r] = zs[b0 + r].T
        return _
    lax.fori_loop(0, 8, ln_step, 0)
    norm_blocks(y, ub, chunk_base(7), 4)
    wcopy(0).wait()
    wbs8[...] = head_rows(wbs[...])
    bias_rows(wbs8[...], ub, bsend)
    ball[:, pl.ds(pl.multiple_of(core * rows, rows), rows)] = bsend[...]
    pl.semaphore_wait(bar, 3)

    def bias_copy(k, t, owner):
        return remote(bsend, ball.at[:, pl.ds(pl.multiple_of((half if k < 2 else 0) + owner % 2 * rows, rows), rows)],
                      bs_s.at[k], bs_r.at[owner], t)

    def end_bias_copy(k, t, owner):
        return remote(besend, beall.at[:, pl.ds(pl.multiple_of(owner * rows, rows), rows)], be_s.at[k], be_r.at[owner], t)

    for k in (2, 0, 1):
        bias_copy(k, peers[k], sp).start()

    for i in range(1, 8):
        wcopy(i).wait()
    wqst[...] = wqs[...].T
    last = npair - 1

    def lag(t, by):
        return jnp.clip(t - by, 0, last)

    def proj_step(p, _):
        for pair in range(heads // 2):
            knp[jnp.maximum(p - 1, 0), pair] = ktp[pair].T
        pair_project(wqst, ub, qb, ktp, vst, gb, p, npair, heads)
        return _

    def start_bias(side):
        for h in range(heads):
            rws = ball[h, side * half:(side + 1) * half].astype(F32)
            tr = jnp.concatenate([rws, rws], axis=0).T * LOG2E
            if side:
                tr = jnp.concatenate([tr[half:], tr[:half]], axis=0)
            biasp[side, :, h * n:(h + 1) * n] = tr

    def start_step(t, _):
        b = lag(t, 3) * 2
        for r in range(2):
            ub[b + r] = norm_t(z1[b + r].astype(BF).astype(F32).T)
        b = lag(t, 2) * 2
        upd = dot_tn(jnp.concatenate([ogb[b], ogb[b + 1]], axis=1), wos[...])
        z1[b] = zs[b] + upd[:n]
        z1[b + 1] = zs[b + 1] + upd[n:]
        b = lag(t, 1) * 2
        for r in range(2):
            block_mix(s, r, biasp, b // npair, vst, gb, ogb, b + r, b % npair + r, heads)
        b = lag(t, 0) * 2
        for r in range(2):
            block_scores(knp, qb, s, r, b + r, b % npair + r, heads)
        return _

    chunks = 4
    cols = rows // chunks
    groups = [(0, 8), (8, 8), (16, 16)]
    near = [(0, 16), (16, 16)]

    def h_copy(gi, ch, k, t, owner):
        r0, size = groups[gi]
        return remote(hsend.at[0, pl.ds(t % 2 * rows + ch * cols, cols), r0:r0 + size],
                      hcol.at[pl.ds(ch * cols, cols), pl.ds(pl.multiple_of(owner * rows + r0, 8), size)],
                      h_s.at[gi, ch, k], h_r.at[gi, ch, owner], t)

    def near_copy(gi, owner):
        r0, size = near[gi]
        return remote(hsend.at[1, pl.ds(pl.multiple_of((1 - core) * rows, rows), rows), r0:r0 + size],
                      hcol.at[:, pl.ds(pl.multiple_of(owner * rows + r0, 8), size)],
                      o_s.at[gi], o_r.at[gi], peers[2])

    def shuffle_rows(side, r0, size):
        def body(jb, _):
            j0 = pl.multiple_of(jb * 8, 8)
            parts = []
            for q in range(r0 // 8, (r0 + size) // 8):
                for i in range(2):
                    parts.append(z1[side * npair + 4 * q:side * npair + 4 * q + 4, pl.ds(i * half + j0, 8)])
            blk = jnp.swapaxes(jnp.concatenate(parts, axis=0), 0, 1)
            hsend[side, pl.ds(j0, 8), r0:r0 + size] = blk.astype(BF)
            return _
        lax.fori_loop(0, half // 8, body, 0)

    def send_h(gi, chs):
        for ch in chs:
            for k in range(2):
                h_copy(gi, ch, k, peers[k], sp).start()

    def turn_keys_of(p):
        for pair in range(heads // 2):
            knp[p, pair] = ktp[pair].T

    lax.fori_loop(0, npair // 2, proj_step, 0, unroll=2)
    turn_keys_of(npair // 2 - 1)
    bias_copy(2, peers[2], peers[2]).wait_recv()
    start_bias(0)
    lax.fori_loop(0, 4, start_step, 0, unroll=2)
    shuffle_rows(0, 0, 8)
    send_h(0, range(chunks))
    lax.fori_loop(npair // 2, npair, proj_step, 0, unroll=2)
    turn_keys_of(last)
    lax.fori_loop(4, 6, start_step, 0, unroll=2)
    shuffle_rows(0, 8, 8)
    send_h(1, range(chunks))
    for k in range(2):
        bias_copy(k, peers[k], peers[k]).wait_recv()
    start_bias(1)
    lax.fori_loop(6, 10, start_step, 0, unroll=2)
    shuffle_rows(0, 16, 16)
    send_h(2, [0])
    lax.fori_loop(10, 14, start_step, 0, unroll=2)
    shuffle_rows(1, 0, 16)
    near_copy(0, sp).start()
    lax.fori_loop(14, 18, start_step, 0, unroll=2)
    for r in range(2):
        ub[rows - 2 + r] = norm_t(z1[rows - 2 + r].astype(BF).astype(F32).T)
    wbe8[...] = head_rows(wbe[...])
    bias_rows(wbe8[...], ub, besend, x == 1)
    for k in range(3):
        end_bias_copy(k, peers[k], sp).start()
    send_h(2, range(1, chunks))
    beall[:, pl.ds(mine, rows)] = besend[...]
    shuffle_rows(1, 16, 16)
    near_copy(1, sp).start()
    hcol[:, pl.ds(mine, rows)] = hsend[1, pl.ds(pl.multiple_of(core * rows, rows), rows)]
    wqet[...] = wqe[...].T
    woet[...] = woe[...].T
    w1t[...] = w1[...].T
    w2t[...] = w2[...].T
    for k in range(3):
        end_bias_copy(k, peers[k], peers[k]).wait_recv()
    for h in range(heads):
        biast[:, h * n:(h + 1) * n] = beall[h].astype(F32) * LOG2E
    for gi in range(2):
        near_copy(gi, peers[2]).wait_recv()

    def end_step(t, _):
        p = lag(t, 4)
        hid = jnp.maximum(dot(w1t[...], u2[p % 2]), 0.0).astype(BF)
        delta = (eb[p % 2] + dot(w2t[...], hid)).astype(BF)
        dsend[2 * p] = delta[:, :n].T
        dsend[2 * p + 1] = delta[:, n:].T
        p = lag(t, 3)
        wt = jnp.concatenate([hcol[2 * p].astype(F32).T, hcol[2 * p + 1].astype(F32).T], axis=1)
        e = dot(woet[...], og[p])
        eb[p % 2] = e
        u2[p % 2] = norm_t(wt + e)
        stage_mix(s, biast, qv, g, og, lag(t, 2), heads)
        turn_keys(kt, kn, lag(t, 1))
        stage_scores(kn, qv, s, lag(t, 1), heads)
        p = lag(t, 0)
        wt = jnp.concatenate([hcol[2 * p].astype(F32).T, hcol[2 * p + 1].astype(F32).T], axis=1)
        project(wqet, norm_t(wt), n, qv, kt, g, p)
        return _

    pieces = 8
    pc = rows // pieces

    def d_copy(q, k, t, owner, first_col):
        return remote(dsend.at[pl.ds(q * pc, pc), pl.ds(pl.multiple_of(t * rows, rows), rows)],
                      drecv.at[pl.ds(first_col + q * pc, pc)], d_s.at[q, k], d_r.at[q, owner], t)

    my_cols = pl.multiple_of((2 * (1 - x) + core) * rows, rows)

    def segment(i, _):
        @pl.when(i % 2 + 8 * (i // pieces) == 0)
        def _wait():
            for gi in range(len(groups)):
                for k in range(2):
                    h_copy(gi, i // 2, k, peers[k], peers[k]).wait_recv()
        end_step(2 * i, 0)
        end_step(2 * i + 1, 0)

        @pl.when(i >= 2)
        def _send():
            for k, t in enumerate(peers):
                d_copy(i - 2, k, t, sp, my_cols).start()
        return _
    lax.fori_loop(0, pieces + 2, segment, 0)
    drecv[pl.ds(my_cols, rows)] = dsend[:, pl.ds(mine, rows)]

    def final_block(side, owner_core, first_col, ch):
        j0 = pl.multiple_of(first_col + ch * cols, 8)
        jj = owner_core * rows + ch * cols
        for gi in range(rows // 16):
            blk = jnp.swapaxes(drecv[pl.ds(j0, 8), gi * 16:(gi + 1) * 16].astype(F32), 0, 1)
            for q in range(2):
                for i in range(2):
                    b0 = side * npair + 4 * (2 * gi + q)
                    part = z1[b0:b0 + 4, pl.ds(pl.multiple_of(i * half + jj, 8), 8)]
                    r0 = 8 * (2 * gi + q) + 4 * i
                    y[r0:r0 + 4, pl.ds(j0, 8)] = part + blk[8 * q + 4 * i:8 * q + 4 * i + 4]

    for ch in range(chunks):
        final_block(1, core, my_cols, ch)
    for ch in range(chunks):
        for k in (2, 0, 1):
            t = peers[k]
            first_col = pl.multiple_of((2 * x + t % 2 if k < 2 else 2 * (1 - x) + t % 2) * rows, rows)
            for q in range(ch * pieces // chunks, (ch + 1) * pieces // chunks):
                d_copy(q, k, t, t, first_col).wait_recv()
            final_block(0 if k < 2 else 1, t % 2, first_col, ch)
    for k, t in enumerate(peers):
        bias_copy(k, t, sp).wait_send()
        end_bias_copy(k, t, sp).wait_send()
        for ch in range(chunks):
            for gi in range(len(groups)):
                if k < 2:
                    h_copy(gi, ch, k, t, sp).wait_send()
        for q in range(pieces):
            d_copy(q, k, t, sp, my_cols).wait_send()
    for gi in range(2):
        near_copy(gi, sp).wait_send()


def solution(mesh):
    row_spec = P(('dp', 'sp'), None, None)
    sp = mesh.shape['sp']

    def local_fn(pair_loc, wqs, wbs, wos, wqe, wbe, woe, w1, w2):
        rows, n, c = pair_loc.shape
        heads = wbs.shape[0]
        dma = pltpu.SemaphoreType.DMA
        vm = pltpu.VMEM
        weights = (wqs, wbs, wos, wqe, wbe, woe, w1, w2)
        npair = rows // 2
        args = (pair_loc.reshape(rows // 8, 2, 4, n, c),) + weights
        return pl.pallas_call(
            kernel,
            out_shape=vm(pair_loc.shape, F32),
            in_specs=[pl.BlockSpec(memory_space=pltpu.HBM)] * 9,
            out_specs=pl.BlockSpec(memory_space=vm),
            scratch_shapes=[
                vm((rows, n, c), F32), vm((rows, n, c), F32), vm((rows, c, n), BF), vm((rows, c, n), BF),
                vm((npair, 2, c, n), BF), vm((npair, 2, n, c), BF), vm((rows, c, n), F32), vm((rows, c, n), BF),
                vm((heads, rows, n), BF), vm((heads, n, n), BF), vm((2, n, heads * n), F32), vm((2, n // 2, rows, c), BF),
                vm((rows, n, c), BF), vm((npair, 2 * c, 2 * n), BF), vm((rows, n, c), BF), vm((npair, c, 2 * n), F32),
                vm((npair, c, 2 * n), BF), vm((heads, rows, n), BF), vm((heads, n, n), BF), vm((n, heads * n), F32),
                vm((rows, n, c), BF), vm((n, rows, c), BF), vm((2, n, heads * n), F32),
                vm((2, c, 2 * n), F32), vm((2, c, 2 * n), BF), vm((c, 2 * n), BF), vm((2, c, n), BF),
                *[vm(w.shape, BF) for w in weights],
                vm(wqs.shape[::-1], BF), vm(wqe.shape[::-1], BF), vm(woe.shape[::-1], BF),
                vm(w1.shape[::-1], BF), vm(w2.shape[::-1], BF),
                vm((heads * 8, 8 * c), BF), vm((heads * 8, 8 * c), BF),
                dma((8, 2)), dma((8,)), dma((3,)), dma((sp,)), dma((3, 4, 3)), dma((3, 4, sp)), dma((2,)), dma((2,)),
                dma((3,)), dma((sp,)), dma((8, 3)), dma((8, sp)),
            ],
            compiler_params=pltpu.CompilerParams(collective_id=0, has_side_effects=True, vmem_limit_bytes=36 * 2 ** 20),
            name="pair_block",
        )(*[pltpu.with_memory_space_constraint(a, pltpu.HBM) for a in args])

    return jax.shard_map(local_fn, mesh=mesh, in_specs=(row_spec,) + (P(),) * 8, out_specs=row_spec, check_vma=False)
```

profile of v0, /device:TPU:0, one launch (start us, length us, event | category | flops | bytes accessed | tf_op | source)
XLA Modules:
  0.0 38.7 jit_solution(15513261142418953796)
XLA Ops:
  0.0 37.4 %pair_block.1 = f32[32,128,128]{2,1,0:T(8,128)S(1)} custom-call(f32[4,2,4,128,128]{4,3,2,1,0:T(8,128)} %bitcast.1, bf16[128,512]{1,0:T(8,128)(2,1)} %wqs_h.1, bf16[4,128]{1,0:T(4,128)(2,1)} %wbs_h.1, bf16[128,128]{1,0:T(8,128)(2,1)} %wos_h.1, bf16[128,512]{1,0:T(8,128)(2,1)} %wqe_h.1, bf16[4,128]{1,0:T(4,128)(2,1)} %wbe_h.1, bf16[128,128]{1,0:T(8,128)(2,1)} %woe_h.1, ...), custom_call_target="tpu_custom_call" | custom-call | tf_op jit(solution)/shard_map/pair_block/pallas_call | solution.py:455
  37.4 1.3 %copy.11 = f32[32,128,128]{2,1,0:T(8,128)} copy(f32[32,128,128]{2,1,0:T(8,128)S(1)} %pair_block.1) | data formatting | bytes 4194304
where the time goes:
time: 38.8 us; the launch traced here: 38.7 us
  Pallas kernels  37.4 us (96%)
  local copies, waits for them, and re-layouts  1.32 us (3%)
    pallas_call x1, Pallas kernels, local_fn(): pl.pallas_call(kernel, out_shape=vm(pair_loc.shape, F32), in_specs=[pl.Bl...  37.4 us
    unnamed x1, local copies, waits for them, and re-layouts  1.32 us

commit v1 on v0

v1 whole, which is shorter than its diff:
```python
import functools

import jax
import jax.numpy as jnp
from jax import lax
from jax.experimental import pallas as pl
from jax.experimental.pallas import tpu as pltpu
from jax.sharding import PartitionSpec as P

MESH = pl.DeviceIdType.MESH
EPS = 1e-5
LOG2E = 1.4426950408889634
BF = jnp.bfloat16
F32 = jnp.float32


def dot(a, b):
    return jnp.dot(a, b, preferred_element_type=F32)


def dot_tn(a, b):
    return lax.dot_general(a, b, (((0,), (0,)), ((), ())), preferred_element_type=F32)


def norm_t(xt):
    mean = jnp.sum(xt, axis=0, keepdims=True) * (1.0 / xt.shape[0])
    cen = xt - mean
    var = jnp.sum(cen * cen, axis=0, keepdims=True) * (1.0 / xt.shape[0])
    return (cen * lax.rsqrt(var + EPS)).astype(BF)


def sigmoid(x):
    return 0.5 * jnp.tanh(0.5 * x) + 0.5


def block_diag(qt, pair, heads):
    hd, n = qt.shape
    d = hd // heads
    cols = []
    for h in (2 * pair, 2 * pair + 1):
        parts = []
        if h:
            parts.append(jnp.zeros((h * d, n), BF))
        parts.append(qt[h * d:(h + 1) * d])
        if h < heads - 1:
            parts.append(jnp.zeros(((heads - 1 - h) * d, n), BF))
        cols.append(jnp.concatenate(parts, axis=0))
    return jnp.concatenate(cols, axis=1)


def stage_scores(kn, qv, s, p, heads):
    c, n = kn.shape[1:]
    for r in range(2):
        keys = kn[2 * p + r]
        qt = qv[p, :c, r * n:(r + 1) * n]
        for pair in range(heads // 2):
            s[r, :, 2 * pair * n:(2 * pair + 2) * n] = dot(keys, block_diag(qt, pair, heads))


def stage_mix(s, biast, qv, g, og, p, heads):
    n = s.shape[1]
    c = qv.shape[1] // 2
    d = c // heads
    scale = LOG2E * d ** -0.5
    for r in range(2):
        for pair in range(heads // 2):
            probs = []
            for h in (2 * pair, 2 * pair + 1):
                t = s[r, :, h * n:(h + 1) * n] * scale + biast[:, h * n:(h + 1) * n]
                e = jnp.exp2(t - jnp.max(t, axis=0, keepdims=True))
                probs.append((e * (1.0 / jnp.sum(e, axis=0, keepdims=True))).astype(BF))
            rows = slice(c + 2 * pair * d, c + (2 * pair + 2) * d)
            o = dot(qv[p, rows, r * n:(r + 1) * n], jnp.concatenate(probs, axis=1))
            for i in range(2):
                h = 2 * pair + i
                out = o[i * d:(i + 1) * d, i * n:(i + 1) * n] * g[p, h * d:(h + 1) * d, r * n:(r + 1) * n]
                og[p, h * d:(h + 1) * d, r * n:(r + 1) * n] = out.astype(BF)


def norm_blocks(src, ut, b0, count):
    for r in range(count):
        ut[b0 + r] = norm_t(src[b0 + r])


def head_rows(wb):
    heads, c = wb.shape
    rep = jnp.broadcast_to(wb.astype(F32)[:, None, :], (heads, 16, c)).reshape(heads * 16, c)
    row = lax.broadcasted_iota(jnp.int32, rep.shape, 0) % 16 // 2
    return jnp.concatenate([jnp.where(row == j, rep, 0.0) for j in range(8)], axis=1).astype(BF)


def bias_rows(w8, ub, dst, i, swap=None):
    heads, rows, n = dst.shape
    c = ub.shape[1]
    half = n // 2
    r0, r1 = [dot(w8, ub[s * rows // 2 + 8 * i:s * rows // 2 + 8 * i + 8].reshape(8 * c, n)) for s in range(2)]
    first, second = [(r0[:, lane:lane + half], r1[:, lane:lane + half]) for lane in (0, half)]
    even = lax.broadcasted_iota(jnp.int32, r0.shape, 0) % 2 == 0
    res = jnp.where(even, jnp.concatenate(first, axis=1), jnp.concatenate(second, axis=1))
    if swap is not None:
        res = jnp.where(swap, jnp.concatenate([res[:, half:], res[:, :half]], axis=1), res)
    dst[:, 16 * i:16 * i + 16] = res.reshape(heads, 16, n).astype(BF)


def low_half(shape):
    return lax.broadcasted_iota(jnp.int32, shape, 1) < shape[1] // 2


def pair_project(wt, ub, qb, kt_ref, vst, g, p, npair, heads):
    own, oth = ub[p], ub[npair + p]
    c, n = own.shape
    d, half = c // heads, n // 2
    u = jnp.concatenate([own, oth], axis=1)
    q = dot(wt[0:c], u).astype(BF)
    qb[p] = q[:, :n]
    qb[npair + p] = q[:, n:]
    u_row = jnp.concatenate([own[:, :half], oth[:, :half], own[:, half:], oth[:, half:]], axis=1)
    k = dot(wt[c:2 * c], u_row).astype(BF)
    v = dot(wt[2 * c:3 * c], u_row).astype(BF)
    for h in range(heads):
        for i in range(2):
            rows = pl.ds((h % 2) * 2 * d + i * d, d)
            kt_ref[h // 2, rows] = k[h * d:(h + 1) * d, i * n:(i + 1) * n]
            vst[p, h // 2, rows] = v[h * d:(h + 1) * d, i * n:(i + 1) * n]
    gate = sigmoid(dot(wt[3 * c:], u))
    g[p] = gate[:, :n]
    g[npair + p] = gate[:, n:]


def block_scores(kn, qb, s, slot, b, p, heads):
    c, n = qb.shape[1:]
    d = c // heads
    low = low_half((d, n))
    zero = jnp.zeros((d, n), BF)
    for pair in range(heads // 2):
        rows = []
        for i in range(2):
            q = qb[b, (2 * pair + i) * d:(2 * pair + i + 1) * d]
            for part in (jnp.where(low, q, zero), jnp.where(low, zero, q)):
                rows.append(jnp.concatenate([part, zero] if i == 0 else [zero, part], axis=1))
        s[slot, :, 2 * pair * n:(2 * pair + 2) * n] = dot(kn[p, pair], jnp.concatenate(rows, axis=0))


def softmax_t(t):
    e = jnp.exp2(t - jnp.max(t, axis=0, keepdims=True))
    return (e * (1.0 / jnp.sum(e, axis=0, keepdims=True))).astype(BF)


def block_mix(s, slot, biast, side, vst, g, og, b, p, heads):
    c, n = og.shape[1:]
    d = c // heads
    low = low_half((d, n))
    for h in range(heads):
        t = s[slot, :, h * n:(h + 1) * n] * (LOG2E * d ** -0.5) + biast[side, :, h * n:(h + 1) * n]
        o = dot(vst[p, h // 2, (h % 2) * 2 * d:(h % 2 + 1) * 2 * d], softmax_t(t))
        og[b, h * d:(h + 1) * d] = (jnp.where(low, o[:d], o[d:]) * g[b, h * d:(h + 1) * d]).astype(BF)


def project(wt, u, n, qv_ref, kt_ref, g_ref, p):
    c = u.shape[0]
    qv_ref[p, :c] = dot(wt[0:c], u).astype(BF)
    kt_ref[...] = dot(wt[c:2 * c], u).astype(BF)
    qv_ref[p, c:] = dot(wt[2 * c:3 * c], u).astype(BF)
    g_ref[p] = sigmoid(dot(wt[3 * c:], u))


def turn_keys(kt_ref, kn_ref, p):
    n = kn_ref.shape[1]
    kn_ref[2 * p] = kt_ref[:, :n].T
    kn_ref[2 * p + 1] = kt_ref[:, n:].T


def kernel(z_hbm, wqs_h, wbs_h, wos_h, wqe_h, wbe_h, woe_h, w1_h, w2_h, y,
           zs4, z1, ub, qb, vst, knp, gb, ogb, bsend, ball, biasp, hsend,
           hcol, qv, kn, g, og, besend, beall, biast, dsend, drecv, s, eb, u2, kt, ktp,
           wqs, wbs, wos, wqe, wbe, woe, w1, w2, wqst, wqet, woet, w1t, w2t, wbs8, wbe8,
           zsem, wsem, bs_s, bs_r, h_s, h_r, o_s, o_r, be_s, be_r, d_s, d_r):
    rows, n, c = y.shape
    npair = rows // 2
    half = n // 2
    heads = wbs.shape[0]
    dp, sp = lax.axis_index("dp"), lax.axis_index("sp")
    x, core = sp // 2, sp % 2
    peers = [2 * (1 - x) + core, 2 * (1 - x) + 1 - core, 2 * x + 1 - core]
    mine = pl.multiple_of(sp * rows, rows)

    def zcopy(ci):
        q, side = ci // 2, ci % 2
        return pltpu.make_async_copy(z_hbm.at[pl.ds(4 * q, 4), :, (x + side) % 2],
                                     zs4.at[pl.ds(side * npair + 4 * q, 4)], zsem.at[ci])

    def wcopy(i):
        src = (wbs_h, wqs_h, wqe_h, woe_h, w1_h, w2_h, wbe_h, wos_h)[i]
        return pltpu.make_async_copy(src, (wbs, wqs, wqe, woe, w1, w2, wbe, wos)[i], wsem.at[i])

    wcopy(0).start()
    wcopy(6).start()
    for ci in range(8):
        zcopy(ci).start()
    for i in (1, 7, 2, 3, 4, 5):
        wcopy(i).start()
    bar = pltpu.get_barrier_semaphore()
    for t in peers:
        pl.semaphore_signal(bar, inc=1, device_id=(dp, t), device_id_type=MESH)

    def remote(src, dst, ssem, rsem, t):
        return pltpu.make_async_remote_copy(src, dst, ssem, rsem, device_id=(dp, t), device_id_type=MESH)

    wcopy(0).wait()
    wcopy(6).wait()
    wbs8[...] = head_rows(wbs[...])
    wbe8[...] = head_rows(wbe[...])

    def chunk_base(ci):
        return ci % 2 * npair + ci // 2 * 4

    def ln_step(ci, _):
        for side in range(2):
            zcopy(2 * ci + side).wait()
        for side in range(2):
            norm_blocks(y, ub, chunk_base(jnp.maximum(2 * ci - 2, 0) + side), 4)
        for side in range(2):
            b0 = chunk_base(2 * ci + side)
            for r in range(4):
                y[b0 + r] = zs4[b0 + r].reshape(n, c).T
        return _
    lax.fori_loop(0, 4, ln_step, 0)
    bias_rows(wbs8[...], ub, bsend, 0)
    for side in range(2):
        norm_blocks(y, ub, chunk_base(6 + side), 4)
    for i in range(1, rows // 16):
        bias_rows(wbs8[...], ub, bsend, i)
    ball[:, pl.ds(pl.multiple_of(core * rows, rows), rows)] = bsend[...]
    pl.semaphore_wait(bar, 3)

    def bias_copy(k, t, owner):
        return remote(bsend, ball.at[:, pl.ds(pl.multiple_of((half if k < 2 else 0) + owner % 2 * rows, rows), rows)],
                      bs_s, bs_r.at[k // 2], t)

    def end_bias_copy(i, t):
        return remote(besend.at[:, 16 * i:16 * i + 16], beall.at[:, pl.ds(pl.multiple_of(mine + 16 * i, 16), 16)], be_s, be_r, t)

    def sent(ref, sem):
        remote(ref, ref, sem, sem, peers[0]).wait_send()

    def arrived(ref, sem):
        remote(ref, ref, sem, sem, peers[0]).wait_recv()

    for k in (2, 0, 1):
        bias_copy(k, peers[k], sp).start()

    wcopy(1).wait()
    wcopy(7).wait()
    wqst[...] = wqs[...].T
    def start_project(*pairs):
        for p in pairs:
            pair_project(wqst, ub, qb, ktp.at[p % 2], vst, gb, p, npair, heads)
        for p in pairs:
            for pair in range(heads // 2):
                knp[p, pair] = ktp[p % 2, pair].T

    def start_bias(side):
        for h in range(heads):
            rws = ball[h, side * half:(side + 1) * half].astype(F32)
            tr = jnp.concatenate([rws, rws], axis=0).T * LOG2E
            if side:
                tr = jnp.concatenate([tr[half:], tr[:half]], axis=0)
            biasp[side, :, h * n:(h + 1) * n] = tr

    def start_out(b):
        upd = dot_tn(jnp.concatenate([ogb[b], ogb[b + 1]], axis=1), wos[...])
        z1[b] = zs4[b].reshape(n, c) + upd[:n]
        z1[b + 1] = zs4[b + 1].reshape(n, c) + upd[n:]
    def start_norm(b):
        for r in range(2):
            ub[b + r] = norm_t(z1[b + r].astype(BF).astype(F32).T)

    def start_mix(b):
        for r in range(2):
            block_mix(s, r, biasp, b // npair, vst, gb, ogb, b + r, b % npair + r, heads)

    def start_scores(b):
        for r in range(2):
            block_scores(knp, qb, s, r, b + r, b % npair + r, heads)

    def start_step(t, _):
        for by, stage in ((3, start_norm), (2, start_out), (1, start_mix), (0, start_scores)):
            if not isinstance(t, int) or 0 <= t - by < npair:
                stage(2 * (t - by))
        return _

    chunks = 4
    cols = rows // chunks
    groups = [(0, 8), (8, 8), (16, 16)]
    near = [(0, 16), (16, 16)]

    def h_copy(gi, ch, k, t, owner):
        r0, size = groups[gi]
        return remote(hsend.at[0, pl.ds(t % 2 * rows + ch * cols, cols), r0:r0 + size],
                      hcol.at[pl.ds(ch * cols, cols), pl.ds(pl.multiple_of(owner * rows + r0, 8), size)],
                      h_s, h_r.at[ch], t)

    def near_copy(gi, owner):
        r0, size = near[gi]
        return remote(hsend.at[1, pl.ds(pl.multiple_of((1 - core) * rows, rows), rows), r0:r0 + size],
                      hcol.at[:, pl.ds(pl.multiple_of(owner * rows + r0, 8), size)],
                      o_s, o_r, peers[2])

    def shuffle_rows(side, r0, size):
        def body(jb, _):
            j0 = pl.multiple_of(jb * 8, 8)
            parts = []
            for row in range(r0, r0 + size):
                b = side * npair + row // 2
                parts.append(z1[b:b + 1, pl.ds(row % 2 * half + j0, 8)])
            blk = jnp.swapaxes(jnp.concatenate(parts, axis=0), 0, 1)
            hsend[side, pl.ds(j0, 8), r0:r0 + size] = blk.astype(BF)
            return _
        lax.fori_loop(0, half // 8, body, 0)

    def send_h(gi, chs):
        for ch in chs:
            for k in range(2):
                h_copy(gi, ch, k, peers[k], sp).start()

    start_project(0, 1)
    start_project(2, 3)
    arrived(ball.at[:, 0:rows], bs_r.at[1])
    start_bias(0)
    start_scores(0)
    start_mix(0)
    start_scores(2)
    start_out(0)
    start_mix(2)
    start_out(2)
    shuffle_rows(0, 0, 8)
    send_h(0, range(chunks))
    start_project(4, 5)
    start_scores(4)
    start_project(6, 7)
    start_norm(0)
    start_mix(4)
    start_scores(6)
    start_project(8, 9)
    start_norm(2)
    start_out(4)
    start_mix(6)
    start_scores(8)
    start_project(10, 11)
    start_step(5, 0)
    shuffle_rows(0, 8, 8)
    send_h(1, range(chunks))
    arrived(ball.at[:, 0:2 * rows], bs_r.at[0])
    start_bias(1)
    for t in (6, 7):
        start_project(2 * t, 2 * t + 1)
        start_step(t, 0)
    for t in (8, 9):
        start_step(t, 0)
    shuffle_rows(0, 16, 16)
    send_h(2, [0])
    h_copy(2, 1, 0, peers[0], sp).start()
    lax.fori_loop(10, 14, start_step, 0, unroll=4)
    shuffle_rows(1, 0, 16)
    near_copy(0, sp).start()
    start_step(14, 0)
    bias_rows(wbe8[...], ub, besend, 0, x == 1)
    for k in range(3):
        end_bias_copy(0, peers[k]).start()
    for t in range(15, npair + 3):
        start_step(t, 0)
    bias_rows(wbe8[...], ub, besend, 1, x == 1)
    for k in range(3):
        end_bias_copy(1, peers[k]).start()
    h_copy(2, 1, 1, peers[1], sp).start()
    beall[:, pl.ds(mine, rows)] = besend[...]
    shuffle_rows(1, 16, 16)
    near_copy(1, sp).start()
    hcol[:, pl.ds(mine, rows)] = hsend[1, pl.ds(pl.multiple_of(core * rows, rows), rows)]
    for i in range(2, 6):
        wcopy(i).wait()
    wqet[...] = wqe[...].T
    woet[...] = woe[...].T
    w1t[...] = w1[...].T
    w2t[...] = w2[...].T
    sent(ball.at[:, 0:3 * rows], bs_s)

    def end_delta(p):
        hid = jnp.maximum(dot(w1t[...], u2[p % 2]), 0.0).astype(BF)
        delta = (eb[p % 2] + dot(w2t[...], hid)).astype(BF)
        dsend[2 * p] = delta[:, :n].T
        dsend[2 * p + 1] = delta[:, n:].T

    def columns(p):
        return jnp.concatenate([hcol[2 * p].astype(F32).T, hcol[2 * p + 1].astype(F32).T], axis=1)

    def end_out(p):
        e = dot(woet[...], og[p])
        eb[p % 2] = e
        u2[p % 2] = norm_t(columns(p) + e)

    def end_mix(p):
        stage_mix(s, biast, qv, g, og, p, heads)

    def end_scores(p):
        turn_keys(kt, kn, p)
        stage_scores(kn, qv, s, p, heads)

    def end_project(p):
        project(wqet, norm_t(columns(p)), n, qv, kt, g, p)

    def end_step(t):
        for by, stage in ((4, end_delta), (3, end_out), (2, end_mix), (1, end_scores), (0, end_project)):
            if not isinstance(t, int) or 0 <= t - by < npair:
                stage(t - by)

    def d_copy(q, count, t, first_col):
        return remote(dsend.at[pl.ds(2 * q, 2 * count), pl.ds(pl.multiple_of(t * rows, rows), rows)],
                      drecv.at[pl.ds(first_col + 2 * q, 2 * count)], d_s, d_r.at[q // (npair // chunks)], t)

    my_cols = pl.multiple_of((2 * (1 - x) + core) * rows, rows)

    def send_d(q, count):
        for t in peers:
            d_copy(q, count, t, my_cols).start()

    def wait_h(ch):
        arrived(hcol.at[pl.ds(ch * cols, cols), 0:2 * rows], h_r.at[ch])

    sent(ball.at[:, 0:3 * rows], be_s)
    send_h(2, [2])
    arrived(hcol.at[:, 0:rows], o_r)
    wait_h(0)
    end_step(0)
    end_step(1)
    send_h(2, [3])
    arrived(beall.at[:, 0:3 * rows], be_r)
    for h in range(heads):
        biast[:, h * n:(h + 1) * n] = beall[h].astype(F32) * LOG2E
    end_step(2)
    end_step(3)

    def segment(i, _):
        @pl.when(i % 2 == 0)
        def _wait():
            wait_h(i // 2)
        end_step(2 * i)
        send_d(2 * i - 4, 1)
        end_step(2 * i + 1)
        send_d(2 * i - 3, 1)
        return _
    lax.fori_loop(2, npair // 2, segment, 0)
    for t in range(npair, npair + 4):
        end_step(t)
        send_d(t - 4, 1)
    drecv[pl.ds(my_cols, rows)] = dsend[:, pl.ds(mine, rows)]

    def final_block(side, owner_core, first_col, ch):
        j0 = pl.multiple_of(first_col + ch * cols, 8)
        jj = owner_core * rows + ch * cols
        for gi in range(rows // 16):
            blk = jnp.swapaxes(drecv[pl.ds(j0, 8), gi * 16:(gi + 1) * 16].astype(F32), 0, 1)
            for r in range(16):
                row = 16 * gi + r
                part = z1[side * npair + row // 2, pl.ds(pl.multiple_of(row % 2 * half + jj, 8), 8)]
                y[row, pl.ds(j0, 8)] = part + blk[r]

    for ch in range(chunks):
        final_block(1, core, my_cols, ch)
    for ch in range(chunks):
        arrived(drecv.at[0:3 * cols], d_r.at[ch])
        for k in (2, 0, 1):
            t = peers[k]
            first_col = pl.multiple_of((2 * x + t % 2 if k < 2 else 2 * (1 - x) + t % 2) * rows, rows)
            final_block(0 if k < 2 else 1, t % 2, first_col, ch)
    sent(hsend.at[0], h_s)
    sent(hcol.at[:, 0:rows], o_s)
    sent(dsend.at[:, 0:3 * rows], d_s)


def solution(mesh):
    row_spec = P(('dp', 'sp'), None, None)
    sp = mesh.shape['sp']

    def local_fn(pair_loc, wqs, wbs, wos, wqe, wbe, woe, w1, w2):
        rows, n, c = pair_loc.shape
        heads = wbs.shape[0]
        dma = pltpu.SemaphoreType.DMA
        vm = pltpu.VMEM
        weights = (wqs, wbs, wos, wqe, wbe, woe, w1, w2)
        npair = rows // 2
        args = (pair_loc.reshape(npair, 2, 2, n // 2, c),) + weights
        return pl.pallas_call(
            kernel,
            out_shape=vm(pair_loc.shape, F32),
            in_specs=[pl.BlockSpec(memory_space=pltpu.HBM)] * 9,
            out_specs=pl.BlockSpec(memory_space=vm),
            scratch_shapes=[
                vm((rows, 2, n // 2, c), F32), vm((rows, n, c), F32), vm((rows, c, n), BF), vm((rows, c, n), BF),
                vm((npair, 2, c, n), BF), vm((npair, 2, n, c), BF), vm((rows, c, n), F32), vm((rows, c, n), BF),
                vm((heads, rows, n), BF), vm((heads, n, n), BF), vm((2, n, heads * n), F32), vm((2, n // 2, rows, c), BF),
                vm((rows, n, c), BF), vm((npair, 2 * c, 2 * n), BF), vm((rows, n, c), BF), vm((npair, c, 2 * n), F32),
                vm((npair, c, 2 * n), BF), vm((heads, rows, n), BF), vm((heads, n, n), BF), vm((n, heads * n), F32),
                vm((rows, n, c), BF), vm((n, rows, c), BF), vm((2, n, heads * n), F32),
                vm((2, c, 2 * n), F32), vm((2, c, 2 * n), BF), vm((c, 2 * n), BF), vm((2, 2, c, n), BF),
                *[vm(w.shape, BF) for w in weights],
                vm(wqs.shape[::-1], BF), vm(wqe.shape[::-1], BF), vm(woe.shape[::-1], BF),
                vm(w1.shape[::-1], BF), vm(w2.shape[::-1], BF),
                vm((heads * 16, 8 * c), BF), vm((heads * 16, 8 * c), BF),
                dma((8,)), dma((8,)), dma, dma((2,)), dma, dma((4,)), dma, dma, dma, dma, dma, dma((4,)),
            ],
            compiler_params=pltpu.CompilerParams(collective_id=0, has_side_effects=True, vmem_limit_bytes=36 * 2 ** 20),
            name="pair_block",
        )(*[pltpu.with_memory_space_constraint(a, pltpu.HBM) for a in args])

    return jax.shard_map(local_fn, mesh=mesh, in_specs=(row_spec,) + (P(),) * 8, out_specs=row_spec, check_vma=False)
```

time: 38.8 us -> 34.5 us (0.89)
  Pallas kernels: 37.4 us -> 33.1 us
    pallas_call x1, Pallas kernels: 37.4 us -> 33.1 us  [local_fn(): pl.pallas_call(kernel, out_shape=vm(pair_loc.shape, F32), in_specs=[pl.Bl...]
where the time goes in v1:
time: 34.5 us; the launch traced here: 34.4 us
  Pallas kernels  33.1 us (96%)
  local copies, waits for them, and re-layouts  1.32 us (4%)
    pallas_call x1, Pallas kernels, local_fn(): pl.pallas_call(kernel, out_shape=vm(pair_loc.shape, F32), in_specs=[pl.Bl...  33.1 us
    unnamed x1, local copies, waits for them, and re-layouts  1.32 us

profile of v1, /device:TPU:0, one launch (start us, length us, event | category | flops | bytes accessed | tf_op | source)
XLA Modules:
  0.0 34.4 jit_solution(3469725357736826995)
XLA Ops:
  0.0 33.1 %pair_block.1 = f32[32,128,128]{2,1,0:T(8,128)S(1)} custom-call(f32[16,2,2,64,128]{4,3,2,1,0:T(8,128)} %bitcast.1, bf16[128,512]{1,0:T(8,128)(2,1)} %wqs_h.1, bf16[4,128]{1,0:T(4,128)(2,1)} %wbs_h.1, bf16[128,128]{1,0:T(8,128)(2,1)} %wos_h.1, bf16[128,512]{1,0:T(8,128)(2,1)} %wqe_h.1, bf16[4,128]{1,0:T(4,128)(2,1)} %wbe_h.1, bf16[128,128]{1,0:T(8,128)(2,1)} %woe_h.1, ...), custom_call_target="tpu_custom_call" | custom-call | tf_op jit(solution)/shard_map/pair_block/pallas_call | solution.py:493
  33.1 1.3 %copy.11 = f32[32,128,128]{2,1,0:T(8,128)} copy(f32[32,128,128]{2,1,0:T(8,128)S(1)} %pair_block.1) | data formatting | bytes 4194304

commit v2 on v1

--- a/solution.py
+++ b/solution.py
@@ -237,8 +237,18 @@
         return remote(bsend, ball.at[:, pl.ds(pl.multiple_of((half if k < 2 else 0) + owner % 2 * rows, rows), rows)],
                       bs_s, bs_r.at[k // 2], t)
 
-    def end_bias_copy(i, t):
-        return remote(besend.at[:, 16 * i:16 * i + 16], beall.at[:, pl.ds(pl.multiple_of(mine + 16 * i, 16), 16)], be_s, be_r, t)
+    def end_bias_part(owner, i):
+        return beall.at[:, pl.ds(pl.multiple_of(owner * rows + 16 * i, 16), 16)]
+
+    def end_bias_send(i):
+        part = besend.at[:, 16 * i:16 * i + 16]
+        for k in ((0, 2), range(3))[i]:
+            remote(part, end_bias_part(sp, i), be_s, be_r.at[2 if k == 2 else i], peers[k]).start()
+
+    def end_bias_forward():
+        part = end_bias_part(peers[0], 0)
+        arrived(part, be_r.at[0])
+        remote(part, part, be_s, be_r.at[2], peers[2]).start()
 
     def sent(ref, sem):
         remote(ref, ref, sem, sem, peers[0]).wait_send()
@@ -325,9 +335,9 @@
 
     start_project(0, 1)
     start_project(2, 3)
+    start_scores(0)
     arrived(ball.at[:, 0:rows], bs_r.at[1])
     start_bias(0)
-    start_scores(0)
     start_mix(0)
     start_scores(2)
     start_out(0)
@@ -350,32 +360,29 @@
     start_step(5, 0)
     shuffle_rows(0, 8, 8)
     send_h(1, range(chunks))
-    arrived(ball.at[:, 0:2 * rows], bs_r.at[0])
-    start_bias(1)
     for t in (6, 7):
         start_project(2 * t, 2 * t + 1)
         start_step(t, 0)
-    for t in (8, 9):
-        start_step(t, 0)
+    start_step(8, 0)
+    arrived(ball.at[:, 0:2 * rows], bs_r.at[0])
+    start_bias(1)
+    start_step(9, 0)
     shuffle_rows(0, 16, 16)
     send_h(2, [0])
-    h_copy(2, 1, 0, peers[0], sp).start()
     lax.fori_loop(10, 14, start_step, 0, unroll=4)
     shuffle_rows(1, 0, 16)
     near_copy(0, sp).start()
     start_step(14, 0)
     bias_rows(wbe8[...], ub, besend, 0, x == 1)
-    for k in range(3):
-        end_bias_copy(0, peers[k]).start()
+    end_bias_send(0)
     for t in range(15, npair + 3):
         start_step(t, 0)
     bias_rows(wbe8[...], ub, besend, 1, x == 1)
-    for k in range(3):
-        end_bias_copy(1, peers[k]).start()
-    h_copy(2, 1, 1, peers[1], sp).start()
+    end_bias_send(1)
     beall[:, pl.ds(mine, rows)] = besend[...]
     shuffle_rows(1, 16, 16)
     near_copy(1, sp).start()
+    send_h(2, [1])
     hcol[:, pl.ds(mine, rows)] = hsend[1, pl.ds(pl.multiple_of(core * rows, rows), rows)]
     for i in range(2, 6):
         wcopy(i).wait()
@@ -427,14 +434,15 @@
     def wait_h(ch):
         arrived(hcol.at[pl.ds(ch * cols, cols), 0:2 * rows], h_r.at[ch])
 
-    sent(ball.at[:, 0:3 * rows], be_s)
+    arrived(hcol.at[:, 0:rows], o_r)
     send_h(2, [2])
-    arrived(hcol.at[:, 0:rows], o_r)
+    end_bias_forward()
+    send_h(2, [3])
     wait_h(0)
     end_step(0)
     end_step(1)
-    send_h(2, [3])
-    arrived(beall.at[:, 0:3 * rows], be_r)
+    arrived(beall.at[:, 0:rows], be_r.at[1])
+    arrived(beall.at[:, 0:rows + 16], be_r.at[2])
     for h in range(heads):
         biast[:, h * n:(h + 1) * n] = beall[h].astype(F32) * LOG2E
     end_step(2)
@@ -445,9 +453,8 @@
         def _wait():
             wait_h(i // 2)
         end_step(2 * i)
-        send_d(2 * i - 4, 1)
         end_step(2 * i + 1)
-        send_d(2 * i - 3, 1)
+        send_d(2 * i - 4, 2)
         return _
     lax.fori_loop(2, npair // 2, segment, 0)
     for t in range(npair, npair + 4):
@@ -474,6 +481,7 @@
             first_col = pl.multiple_of((2 * x + t % 2 if k < 2 else 2 * (1 - x) + t % 2) * rows, rows)
             final_block(0 if k < 2 else 1, t % 2, first_col, ch)
     sent(hsend.at[0], h_s)
+    sent(ball.at[:, 0:3 * rows], be_s)
     sent(hcol.at[:, 0:rows], o_s)
     sent(dsend.at[:, 0:3 * rows], d_s)
 
@@ -507,7 +515,7 @@
                 vm(wqs.shape[::-1], BF), vm(wqe.shape[::-1], BF), vm(woe.shape[::-1], BF),
                 vm(w1.shape[::-1], BF), vm(w2.shape[::-1], BF),
                 vm((heads * 16, 8 * c), BF), vm((heads * 16, 8 * c), BF),
-                dma((8,)), dma((8,)), dma, dma((2,)), dma, dma((4,)), dma, dma, dma, dma, dma, dma((4,)),
+                dma((8,)), dma((8,)), dma, dma((2,)), dma, dma((4,)), dma, dma, dma, dma((3,)), dma, dma((4,)),
             ],
             compiler_params=pltpu.CompilerParams(collective_id=0, has_side_effects=True, vmem_limit_bytes=36 * 2 ** 20),
             name="pair_block",

time: 34.5 us -> 34.3 us (level)
  no operation moved by 1% of the time
where the time goes in v2:
time: 34.3 us; the launch traced here: 34.2 us
  Pallas kernels  32.8 us (96%)
  local copies, waits for them, and re-layouts  1.32 us (4%)
    pallas_call x1, Pallas kernels, local_fn(): pl.pallas_call(kernel, out_shape=vm(pair_loc.shape, F32), in_specs=[pl.Bl...  32.8 us
    unnamed x1, local copies, waits for them, and re-layouts  1.32 us

profile of v2, /device:TPU:0, one launch (start us, length us, event | category | flops | bytes accessed | tf_op | source)
XLA Modules:
  0.0 34.2 jit_solution(6396606354857314841)
XLA Ops:
  0.0 32.8 %pair_block.1 = f32[32,128,128]{2,1,0:T(8,128)S(1)} custom-call(f32[16,2,2,64,128]{4,3,2,1,0:T(8,128)} %bitcast.1, bf16[128,512]{1,0:T(8,128)(2,1)} %wqs_h.1, bf16[4,128]{1,0:T(4,128)(2,1)} %wbs_h.1, bf16[128,128]{1,0:T(8,128)(2,1)} %wos_h.1, bf16[128,512]{1,0:T(8,128)(2,1)} %wqe_h.1, bf16[4,128]{1,0:T(4,128)(2,1)} %wbe_h.1, bf16[128,128]{1,0:T(8,128)(2,1)} %woe_h.1, ...), custom_call_target="tpu_custom_call" | custom-call | tf_op jit(solution)/shard_map/pair_block/pallas_call | solution.py:501
  32.9 1.3 %copy.11 = f32[32,128,128]{2,1,0:T(8,128)} copy(f32[32,128,128]{2,1,0:T(8,128)S(1)} %pair_block.1) | data formatting | bytes 4194304

commit v3 on v2

--- a/solution.py
+++ b/solution.py
@@ -9,6 +9,8 @@
 
 MESH = pl.DeviceIdType.MESH
 EPS = 1e-5
+TILE = 8
+GROUP = 16
 LOG2E = 1.4426950408889634
 BF = jnp.bfloat16
 F32 = jnp.float32
@@ -84,22 +86,22 @@
 
 def head_rows(wb):
     heads, c = wb.shape
-    rep = jnp.broadcast_to(wb.astype(F32)[:, None, :], (heads, 16, c)).reshape(heads * 16, c)
-    row = lax.broadcasted_iota(jnp.int32, rep.shape, 0) % 16 // 2
-    return jnp.concatenate([jnp.where(row == j, rep, 0.0) for j in range(8)], axis=1).astype(BF)
+    rep = jnp.broadcast_to(wb.astype(F32)[:, None, :], (heads, GROUP, c)).reshape(heads * GROUP, c)
+    row = lax.broadcasted_iota(jnp.int32, rep.shape, 0) % GROUP // 2
+    return jnp.concatenate([jnp.where(row == j, rep, 0.0) for j in range(TILE)], axis=1).astype(BF)
 
 
 def bias_rows(w8, ub, dst, i, swap=None):
     heads, rows, n = dst.shape
     c = ub.shape[1]
     half = n // 2
-    r0, r1 = [dot(w8, ub[s * rows // 2 + 8 * i:s * rows // 2 + 8 * i + 8].reshape(8 * c, n)) for s in range(2)]
+    r0, r1 = [dot(w8, ub[s * rows // 2 + TILE * i:s * rows // 2 + TILE * i + TILE].reshape(TILE * c, n)) for s in range(2)]
     first, second = [(r0[:, lane:lane + half], r1[:, lane:lane + half]) for lane in (0, half)]
     even = lax.broadcasted_iota(jnp.int32, r0.shape, 0) % 2 == 0
     res = jnp.where(even, jnp.concatenate(first, axis=1), jnp.concatenate(second, axis=1))
     if swap is not None:
         res = jnp.where(swap, jnp.concatenate([res[:, half:], res[:, :half]], axis=1), res)
-    dst[:, 16 * i:16 * i + 16] = res.reshape(heads, 16, n).astype(BF)
+    dst[:, GROUP * i:GROUP * i + GROUP] = res.reshape(heads, GROUP, n).astype(BF)
 
 
 def low_half(shape):
@@ -172,7 +174,7 @@
 
 def kernel(z_hbm, wqs_h, wbs_h, wos_h, wqe_h, wbe_h, woe_h, w1_h, w2_h, y,
            zs4, z1, ub, qb, vst, knp, gb, ogb, bsend, ball, biasp, hsend,
-           hcol, qv, kn, g, og, besend, beall, biast, dsend, drecv, s, eb, u2, kt, ktp,
+           hcol, qv, kn, g, og, besend, beall, biast, dsend, drecv, s, s_next, eb, u2, kt, ktp,
            wqs, wbs, wos, wqe, wbe, woe, w1, w2, wqst, wqet, woet, w1t, w2t, wbs8, wbe8,
            zsem, wsem, bs_s, bs_r, h_s, h_r, o_s, o_r, be_s, be_r, d_s, d_r):
     rows, n, c = y.shape
@@ -195,7 +197,7 @@
 
     wcopy(0).start()
     wcopy(6).start()
-    for ci in range(8):
+    for ci in range(TILE):
         zcopy(ci).start()
     for i in (1, 7, 2, 3, 4, 5):
         wcopy(i).start()
@@ -228,7 +230,7 @@
     bias_rows(wbs8[...], ub, bsend, 0)
     for side in range(2):
         norm_blocks(y, ub, chunk_base(6 + side), 4)
-    for i in range(1, rows // 16):
+    for i in range(1, rows // GROUP):
         bias_rows(wbs8[...], ub, bsend, i)
     ball[:, pl.ds(pl.multiple_of(core * rows, rows), rows)] = bsend[...]
     pl.semaphore_wait(bar, 3)
@@ -238,10 +240,10 @@
                       bs_s, bs_r.at[k // 2], t)
 
     def end_bias_part(owner, i):
-        return beall.at[:, pl.ds(pl.multiple_of(owner * rows + 16 * i, 16), 16)]
+        return beall.at[:, pl.ds(pl.multiple_of(owner * rows + GROUP * i, GROUP), GROUP)]
 
     def end_bias_send(i):
-        part = besend.at[:, 16 * i:16 * i + 16]
+        part = besend.at[:, GROUP * i:GROUP * i + GROUP]
         for k in ((0, 2), range(3))[i]:
             remote(part, end_bias_part(sp, i), be_s, be_r.at[2 if k == 2 else i], peers[k]).start()
 
@@ -285,13 +287,13 @@
         for r in range(2):
             ub[b + r] = norm_t(z1[b + r].astype(BF).astype(F32).T)
 
-    def start_mix(b):
+    def start_mix(b, buf=s):
         for r in range(2):
-            block_mix(s, r, biasp, b // npair, vst, gb, ogb, b + r, b % npair + r, heads)
-
-    def start_scores(b):
+            block_mix(buf, r, biasp, b // npair, vst, gb, ogb, b + r, b % npair + r, heads)
+
+    def start_scores(b, buf=s):
         for r in range(2):
-            block_scores(knp, qb, s, r, b + r, b % npair + r, heads)
+            block_scores(knp, qb, buf, r, b + r, b % npair + r, heads)
 
     def start_step(t, _):
         for by, stage in ((3, start_norm), (2, start_out), (1, start_mix), (0, start_scores)):
@@ -301,32 +303,32 @@
 
     chunks = 4
     cols = rows // chunks
-    groups = [(0, 8), (8, 8), (16, 16)]
-    near = [(0, 16), (16, 16)]
+    groups = [(0, TILE), (TILE, TILE), (GROUP, GROUP)]
+    near = [(0, GROUP), (GROUP, GROUP)]
 
     def h_copy(gi, ch, k, t, owner):
         r0, size = groups[gi]
         return remote(hsend.at[0, pl.ds(t % 2 * rows + ch * cols, cols), r0:r0 + size],
-                      hcol.at[pl.ds(ch * cols, cols), pl.ds(pl.multiple_of(owner * rows + r0, 8), size)],
+                      hcol.at[pl.ds(ch * cols, cols), pl.ds(pl.multiple_of(owner * rows + r0, TILE), size)],
                       h_s, h_r.at[ch], t)
 
     def near_copy(gi, owner):
         r0, size = near[gi]
         return remote(hsend.at[1, pl.ds(pl.multiple_of((1 - core) * rows, rows), rows), r0:r0 + size],
-                      hcol.at[:, pl.ds(pl.multiple_of(owner * rows + r0, 8), size)],
+                      hcol.at[:, pl.ds(pl.multiple_of(owner * rows + r0, TILE), size)],
                       o_s, o_r, peers[2])
 
     def shuffle_rows(side, r0, size):
         def body(jb, _):
-            j0 = pl.multiple_of(jb * 8, 8)
+            j0 = pl.multiple_of(jb * TILE, TILE)
             parts = []
             for row in range(r0, r0 + size):
                 b = side * npair + row // 2
-                parts.append(z1[b:b + 1, pl.ds(row % 2 * half + j0, 8)])
+                parts.append(z1[b:b + 1, pl.ds(row % 2 * half + j0, TILE)])
             blk = jnp.swapaxes(jnp.concatenate(parts, axis=0), 0, 1)
-            hsend[side, pl.ds(j0, 8), r0:r0 + size] = blk.astype(BF)
+            hsend[side, pl.ds(j0, TILE), r0:r0 + size] = blk.astype(BF)
             return _
-        lax.fori_loop(0, half // 8, body, 0)
+        lax.fori_loop(0, half // TILE, body, 0, unroll=2)
 
     def send_h(gi, chs):
         for ch in chs:
@@ -336,14 +338,14 @@
     start_project(0, 1)
     start_project(2, 3)
     start_scores(0)
+    start_scores(2, s_next)
     arrived(ball.at[:, 0:rows], bs_r.at[1])
     start_bias(0)
     start_mix(0)
-    start_scores(2)
+    start_mix(2, s_next)
     start_out(0)
-    start_mix(2)
     start_out(2)
-    shuffle_rows(0, 0, 8)
+    shuffle_rows(0, 0, TILE)
     send_h(0, range(chunks))
     start_project(4, 5)
     start_scores(4)
@@ -351,26 +353,26 @@
     start_norm(0)
     start_mix(4)
     start_scores(6)
-    start_project(8, 9)
+    start_project(TILE, 9)
     start_norm(2)
     start_out(4)
     start_mix(6)
-    start_scores(8)
+    start_scores(TILE)
     start_project(10, 11)
     start_step(5, 0)
-    shuffle_rows(0, 8, 8)
+    shuffle_rows(0, TILE, TILE)
     send_h(1, range(chunks))
     for t in (6, 7):
         start_project(2 * t, 2 * t + 1)
         start_step(t, 0)
-    start_step(8, 0)
+    start_step(TILE, 0)
     arrived(ball.at[:, 0:2 * rows], bs_r.at[0])
     start_bias(1)
     start_step(9, 0)
-    shuffle_rows(0, 16, 16)
+    shuffle_rows(0, GROUP, GROUP)
     send_h(2, [0])
     lax.fori_loop(10, 14, start_step, 0, unroll=4)
-    shuffle_rows(1, 0, 16)
+    shuffle_rows(1, 0, GROUP)
     near_copy(0, sp).start()
     start_step(14, 0)
     bias_rows(wbe8[...], ub, besend, 0, x == 1)
@@ -380,7 +382,7 @@
     bias_rows(wbe8[...], ub, besend, 1, x == 1)
     end_bias_send(1)
     beall[:, pl.ds(mine, rows)] = besend[...]
-    shuffle_rows(1, 16, 16)
+    shuffle_rows(1, GROUP, GROUP)
     near_copy(1, sp).start()
     send_h(2, [1])
     hcol[:, pl.ds(mine, rows)] = hsend[1, pl.ds(pl.multiple_of(core * rows, rows), rows)]
@@ -442,7 +444,7 @@
     end_step(0)
     end_step(1)
     arrived(beall.at[:, 0:rows], be_r.at[1])
-    arrived(beall.at[:, 0:rows + 16], be_r.at[2])
+    arrived(beall.at[:, 0:rows + GROUP], be_r.at[2])
     for h in range(heads):
         biast[:, h * n:(h + 1) * n] = beall[h].astype(F32) * LOG2E
     end_step(2)
@@ -463,14 +465,14 @@
     drecv[pl.ds(my_cols, rows)] = dsend[:, pl.ds(mine, rows)]
 
     def final_block(side, owner_core, first_col, ch):
-        j0 = pl.multiple_of(first_col + ch * cols, 8)
+        j0 = pl.multiple_of(first_col + ch * cols, TILE)
         jj = owner_core * rows + ch * cols
-        for gi in range(rows // 16):
-            blk = jnp.swapaxes(drecv[pl.ds(j0, 8), gi * 16:(gi + 1) * 16].astype(F32), 0, 1)
-            for r in range(16):
-                row = 16 * gi + r
-                part = z1[side * npair + row // 2, pl.ds(pl.multiple_of(row % 2 * half + jj, 8), 8)]
-                y[row, pl.ds(j0, 8)] = part + blk[r]
+        for gi in range(rows // GROUP):
+            blk = jnp.swapaxes(drecv[pl.ds(j0, TILE), gi * GROUP:(gi + 1) * GROUP].astype(F32), 0, 1)
+            for r in range(GROUP):
+                row = GROUP * gi + r
+                part = z1[side * npair + row // 2, pl.ds(pl.multiple_of(row % 2 * half + jj, TILE), TILE)]
+                y[row, pl.ds(j0, TILE)] = part + blk[r]
 
     for ch in range(chunks):
         final_block(1, core, my_cols, ch)
@@ -509,16 +511,16 @@
                 vm((heads, rows, n), BF), vm((heads, n, n), BF), vm((2, n, heads * n), F32), vm((2, n // 2, rows, c), BF),
                 vm((rows, n, c), BF), vm((npair, 2 * c, 2 * n), BF), vm((rows, n, c), BF), vm((npair, c, 2 * n), F32),
                 vm((npair, c, 2 * n), BF), vm((heads, rows, n), BF), vm((heads, n, n), BF), vm((n, heads * n), F32),
-                vm((rows, n, c), BF), vm((n, rows, c), BF), vm((2, n, heads * n), F32),
+                vm((rows, n, c), BF), vm((n, rows, c), BF), vm((2, n, heads * n), F32), vm((2, n, heads * n), F32),
                 vm((2, c, 2 * n), F32), vm((2, c, 2 * n), BF), vm((c, 2 * n), BF), vm((2, 2, c, n), BF),
                 *[vm(w.shape, BF) for w in weights],
                 vm(wqs.shape[::-1], BF), vm(wqe.shape[::-1], BF), vm(woe.shape[::-1], BF),
                 vm(w1.shape[::-1], BF), vm(w2.shape[::-1], BF),
-                vm((heads * 16, 8 * c), BF), vm((heads * 16, 8 * c), BF),
-                dma((8,)), dma((8,)), dma, dma((2,)), dma, dma((4,)), dma, dma, dma, dma((3,)), dma, dma((4,)),
+                vm((heads * GROUP, TILE * c), BF), vm((heads * GROUP, TILE * c), BF),
+                dma((TILE,)), dma((TILE,)), dma, dma((2,)), dma, dma((4,)), dma, dma, dma, dma((3,)), dma, dma((4,)),
             ],
             compiler_params=pltpu.CompilerParams(collective_id=0, has_side_effects=True, vmem_limit_bytes=36 * 2 ** 20),
             name="pair_block",
         )(*[pltpu.with_memory_space_constraint(a, pltpu.HBM) for a in args])
 
-    return jax.shard_map(local_fn, mesh=mesh, in_specs=(row_spec,) + (P(),) * 8, out_specs=row_spec, check_vma=False)
+    return jax.shard_map(local_fn, mesh=mesh, in_specs=(row_spec,) + (P(),) * TILE, out_specs=row_spec, check_vma=False)

time: 34.3 us -> 33.9 us (0.988)
  Pallas kernels: 32.8 us -> 32.4 us
    pallas_call x1, Pallas kernels: 32.8 us -> 32.4 us  [local_fn(): pl.pallas_call(kernel, out_shape=vm(pair_loc.shape, F32), in_specs=[pl.Bl...]
where the time goes in v3:
time: 33.9 us; the launch traced here: 33.8 us
  Pallas kernels  32.4 us (96%)
  local copies, waits for them, and re-layouts  1.32 us (4%)
    pallas_call x1, Pallas kernels, local_fn(): pl.pallas_call(kernel, out_shape=vm(pair_loc.shape, F32), in_specs=[pl.Bl...  32.4 us
    unnamed x1, local copies, waits for them, and re-layouts  1.32 us

profile of v3, /device:TPU:0, one launch (start us, length us, event | category | flops | bytes accessed | tf_op | source)
XLA Modules:
  0.0 33.8 jit_solution(18260830936805072613)
XLA Ops:
  0.0 32.4 %pair_block.1 = f32[32,128,128]{2,1,0:T(8,128)S(1)} custom-call(f32[16,2,2,64,128]{4,3,2,1,0:T(8,128)} %bitcast.1, bf16[128,512]{1,0:T(8,128)(2,1)} %wqs_h.1, bf16[4,128]{1,0:T(4,128)(2,1)} %wbs_h.1, bf16[128,128]{1,0:T(8,128)(2,1)} %wos_h.1, bf16[128,512]{1,0:T(8,128)(2,1)} %wqe_h.1, bf16[4,128]{1,0:T(4,128)(2,1)} %wbe_h.1, bf16[128,128]{1,0:T(8,128)(2,1)} %woe_h.1, ...), custom_call_target="tpu_custom_call" | custom-call | tf_op jit(solution)/shard_map/pair_block/pallas_call | solution.py:503
  32.4 1.3 %copy.11 = f32[32,128,128]{2,1,0:T(8,128)} copy(f32[32,128,128]{2,1,0:T(8,128)S(1)} %pair_block.1) | data formatting | bytes 4194304

commit v4 on v3

--- a/solution.py
+++ b/solution.py
@@ -189,11 +189,11 @@
     def zcopy(ci):
         q, side = ci // 2, ci % 2
         return pltpu.make_async_copy(z_hbm.at[pl.ds(4 * q, 4), :, (x + side) % 2],
-                                     zs4.at[pl.ds(side * npair + 4 * q, 4)], zsem.at[ci])
+                                     zs4.at[pl.ds(side * npair + 4 * q, 4)], zsem.at[q])
 
     def wcopy(i):
         src = (wbs_h, wqs_h, wqe_h, woe_h, w1_h, w2_h, wbe_h, wos_h)[i]
-        return pltpu.make_async_copy(src, (wbs, wqs, wqe, woe, w1, w2, wbe, wos)[i], wsem.at[i])
+        return pltpu.make_async_copy(src, (wbs, wqs, wqe, woe, w1, w2, wbe, wos)[i], wsem.at[(0, 1, 2, 2, 2, 2, 3, 4)[i]])
 
     wcopy(0).start()
     wcopy(6).start()
@@ -208,6 +208,12 @@
     def remote(src, dst, ssem, rsem, t):
         return pltpu.make_async_remote_copy(src, dst, ssem, rsem, device_id=(dp, t), device_id_type=MESH)
 
+    def sent(ref, sem):
+        remote(ref, ref, sem, sem, peers[0]).wait_send()
+
+    def arrived(ref, sem):
+        remote(ref, ref, sem, sem, peers[0]).wait_recv()
+
     wcopy(0).wait()
     wcopy(6).wait()
     wbs8[...] = head_rows(wbs[...])
@@ -216,17 +222,22 @@
     def chunk_base(ci):
         return ci % 2 * npair + ci // 2 * 4
 
-    def ln_step(ci, _):
+    def turn_chunks(q):
+        arrived(zs4.at[0:TILE], zsem.at[q])
         for side in range(2):
-            zcopy(2 * ci + side).wait()
-        for side in range(2):
-            norm_blocks(y, ub, chunk_base(jnp.maximum(2 * ci - 2, 0) + side), 4)
-        for side in range(2):
-            b0 = chunk_base(2 * ci + side)
+            b0 = chunk_base(2 * q + side)
             for r in range(4):
                 y[b0 + r] = zs4[b0 + r].reshape(n, c).T
-        return _
-    lax.fori_loop(0, 4, ln_step, 0)
+
+    def norm_chunks(q):
+        for side in range(2):
+            norm_blocks(y, ub, chunk_base(2 * q + side), 4)
+
+    turn_chunks(0)
+    for q in range(1, 4):
+        turn_chunks(q)
+        norm_chunks(q - 1)
+    norm_chunks(3)
     bias_rows(wbs8[...], ub, bsend, 0)
     for side in range(2):
         norm_blocks(y, ub, chunk_base(6 + side), 4)
@@ -251,12 +262,6 @@
         part = end_bias_part(peers[0], 0)
         arrived(part, be_r.at[0])
         remote(part, part, be_s, be_r.at[2], peers[2]).start()
-
-    def sent(ref, sem):
-        remote(ref, ref, sem, sem, peers[0]).wait_send()
-
-    def arrived(ref, sem):
-        remote(ref, ref, sem, sem, peers[0]).wait_recv()
 
     for k in (2, 0, 1):
         bias_copy(k, peers[k], sp).start()
@@ -273,8 +278,8 @@
 
     def start_bias(side):
         for h in range(heads):
-            rws = ball[h, side * half:(side + 1) * half].astype(F32)
-            tr = jnp.concatenate([rws, rws], axis=0).T * LOG2E
+            rws = ball[h, side * half:(side + 1) * half]
+            tr = jnp.concatenate([rws, rws], axis=0).T.astype(F32) * LOG2E
             if side:
                 tr = jnp.concatenate([tr[half:], tr[:half]], axis=0)
             biasp[side, :, h * n:(h + 1) * n] = tr
@@ -328,7 +333,7 @@
             blk = jnp.swapaxes(jnp.concatenate(parts, axis=0), 0, 1)
             hsend[side, pl.ds(j0, TILE), r0:r0 + size] = blk.astype(BF)
             return _
-        lax.fori_loop(0, half // TILE, body, 0, unroll=2)
+        lax.fori_loop(0, half // TILE, body, 0, unroll=8)
 
     def send_h(gi, chs):
         for ch in chs:
@@ -386,8 +391,7 @@
     near_copy(1, sp).start()
     send_h(2, [1])
     hcol[:, pl.ds(mine, rows)] = hsend[1, pl.ds(pl.multiple_of(core * rows, rows), rows)]
-    for i in range(2, 6):
-        wcopy(i).wait()
+    arrived(hcol.at[0:13], wsem.at[2])
     wqet[...] = wqe[...].T
     woet[...] = woe[...].T
     w1t[...] = w1[...].T
@@ -517,7 +521,7 @@
                 vm(wqs.shape[::-1], BF), vm(wqe.shape[::-1], BF), vm(woe.shape[::-1], BF),
                 vm(w1.shape[::-1], BF), vm(w2.shape[::-1], BF),
                 vm((heads * GROUP, TILE * c), BF), vm((heads * GROUP, TILE * c), BF),
-                dma((TILE,)), dma((TILE,)), dma, dma((2,)), dma, dma((4,)), dma, dma, dma, dma((3,)), dma, dma((4,)),
+                dma((4,)), dma((5,)), dma, dma((2,)), dma, dma((4,)), dma, dma, dma, dma((3,)), dma, dma((4,)),
             ],
             compiler_params=pltpu.CompilerParams(collective_id=0, has_side_effects=True, vmem_limit_bytes=36 * 2 ** 20),
             name="pair_block",

time: 33.9 us -> 33.7 us (level)
  no operation moved by 1% of the time
where the time goes in v4:
time: 33.7 us; the launch traced here: 33.5 us
  Pallas kernels  32.2 us (96%)
  local copies, waits for them, and re-layouts  1.32 us (4%)
    pallas_call x1, Pallas kernels, local_fn(): pl.pallas_call(kernel, out_shape=vm(pair_loc.shape, F32), in_specs=[pl.Bl...  32.2 us
    unnamed x1, local copies, waits for them, and re-layouts  1.32 us

profile of v4, /device:TPU:0, one launch (start us, length us, event | category | flops | bytes accessed | tf_op | source)
XLA Modules:
  0.0 33.5 jit_solution(11936239874876258623)
XLA Ops:
  0.0 32.2 %pair_block.1 = f32[32,128,128]{2,1,0:T(8,128)S(1)} custom-call(f32[16,2,2,64,128]{4,3,2,1,0:T(8,128)} %bitcast.1, bf16[128,512]{1,0:T(8,128)(2,1)} %wqs_h.1, bf16[4,128]{1,0:T(4,128)(2,1)} %wbs_h.1, bf16[128,128]{1,0:T(8,128)(2,1)} %wos_h.1, bf16[128,512]{1,0:T(8,128)(2,1)} %wqe_h.1, bf16[4,128]{1,0:T(4,128)(2,1)} %wbe_h.1, bf16[128,128]{1,0:T(8,128)(2,1)} %woe_h.1, ...), custom_call_target="tpu_custom_call" | custom-call | tf_op jit(solution)/shard_map/pair_block/pallas_call | solution.py:507
  32.2 1.3 %copy.11 = f32[32,128,128]{2,1,0:T(8,128)} copy(f32[32,128,128]{2,1,0:T(8,128)S(1)} %pair_block.1) | data formatting | bytes 4194304

commit v5 on v4

--- a/solution.py
+++ b/solution.py
@@ -427,15 +427,15 @@
             if not isinstance(t, int) or 0 <= t - by < npair:
                 stage(t - by)
 
-    def d_copy(q, count, t, first_col):
+    def d_copy(q, count, k, t, first_col):
         return remote(dsend.at[pl.ds(2 * q, 2 * count), pl.ds(pl.multiple_of(t * rows, rows), rows)],
-                      drecv.at[pl.ds(first_col + 2 * q, 2 * count)], d_s, d_r.at[q // (npair // chunks)], t)
+                      drecv.at[pl.ds(first_col + 2 * q, 2 * count)], d_s, d_r.at[chunks if k == 2 else q // (npair // chunks)], t)
 
     my_cols = pl.multiple_of((2 * (1 - x) + core) * rows, rows)
 
     def send_d(q, count):
-        for t in peers:
-            d_copy(q, count, t, my_cols).start()
+        for k, t in enumerate(peers):
+            d_copy(q, count, k, t, my_cols).start()
 
     def wait_h(ch):
         arrived(hcol.at[pl.ds(ch * cols, cols), 0:2 * rows], h_r.at[ch])
@@ -480,12 +480,13 @@
 
     for ch in range(chunks):
         final_block(1, core, my_cols, ch)
+    arrived(drecv.at[0:rows], d_r.at[chunks])
     for ch in range(chunks):
-        arrived(drecv.at[0:3 * cols], d_r.at[ch])
-        for k in (2, 0, 1):
-            t = peers[k]
-            first_col = pl.multiple_of((2 * x + t % 2 if k < 2 else 2 * (1 - x) + t % 2) * rows, rows)
-            final_block(0 if k < 2 else 1, t % 2, first_col, ch)
+        final_block(1, 1 - core, pl.multiple_of((2 * (1 - x) + 1 - core) * rows, rows), ch)
+    for ch in range(chunks):
+        arrived(drecv.at[0:2 * cols], d_r.at[ch])
+        for t in peers[:2]:
+            final_block(0, t % 2, pl.multiple_of((2 * x + t % 2) * rows, rows), ch)
     sent(hsend.at[0], h_s)
     sent(ball.at[:, 0:3 * rows], be_s)
     sent(hcol.at[:, 0:rows], o_s)
@@ -521,7 +522,7 @@
                 vm(wqs.shape[::-1], BF), vm(wqe.shape[::-1], BF), vm(woe.shape[::-1], BF),
                 vm(w1.shape[::-1], BF), vm(w2.shape[::-1], BF),
                 vm((heads * GROUP, TILE * c), BF), vm((heads * GROUP, TILE * c), BF),
-                dma((4,)), dma((5,)), dma, dma((2,)), dma, dma((4,)), dma, dma, dma, dma((3,)), dma, dma((4,)),
+                dma((4,)), dma((5,)), dma, dma((2,)), dma, dma((4,)), dma, dma, dma, dma((3,)), dma, dma((5,)),
             ],
             compiler_params=pltpu.CompilerParams(collective_id=0, has_side_effects=True, vmem_limit_bytes=36 * 2 ** 20),
             name="pair_block",

time: 33.7 us -> 33.6 us (level)
  no operation moved by 1% of the time
where the time goes in v5:
time: 33.6 us; the launch traced here: 33.5 us
  Pallas kernels  32.2 us (96%)
  local copies, waits for them, and re-layouts  1.32 us (4%)
    pallas_call x1, Pallas kernels, local_fn(): pl.pallas_call(kernel, out_shape=vm(pair_loc.shape, F32), in_specs=[pl.Bl...  32.2 us
    unnamed x1, local copies, waits for them, and re-layouts  1.32 us

profile of v5, /device:TPU:0, one launch (start us, length us, event | category | flops | bytes accessed | tf_op | source)
XLA Modules:
  0.0 33.5 jit_solution(12816602871493316767)
XLA Ops:
  0.0 32.2 %pair_block.1 = f32[32,128,128]{2,1,0:T(8,128)S(1)} custom-call(f32[16,2,2,64,128]{4,3,2,1,0:T(8,128)} %bitcast.1, bf16[128,512]{1,0:T(8,128)(2,1)} %wqs_h.1, bf16[4,128]{1,0:T(4,128)(2,1)} %wbs_h.1, bf16[128,128]{1,0:T(8,128)(2,1)} %wos_h.1, bf16[128,512]{1,0:T(8,128)(2,1)} %wqe_h.1, bf16[4,128]{1,0:T(4,128)(2,1)} %wbe_h.1, bf16[128,128]{1,0:T(8,128)(2,1)} %woe_h.1, ...), custom_call_target="tpu_custom_call" | custom-call | tf_op jit(solution)/shard_map/pair_block/pallas_call | solution.py:508
  32.2 1.3 %copy.11 = f32[32,128,128]{2,1,0:T(8,128)} copy(f32[32,128,128]{2,1,0:T(8,128)S(1)} %pair_block.1) | data formatting | bytes 4194304

commit v6 on v5

--- a/solution.py
+++ b/solution.py
@@ -176,7 +176,7 @@
            zs4, z1, ub, qb, vst, knp, gb, ogb, bsend, ball, biasp, hsend,
            hcol, qv, kn, g, og, besend, beall, biast, dsend, drecv, s, s_next, eb, u2, kt, ktp,
            wqs, wbs, wos, wqe, wbe, woe, w1, w2, wqst, wqet, woet, w1t, w2t, wbs8, wbe8,
-           zsem, wsem, bs_s, bs_r, h_s, h_r, o_s, o_r, be_s, be_r, d_s, d_r):
+           zsem, wsem, out_s, bs_r, h_r, o_r, be_r, d_r):
     rows, n, c = y.shape
     npair = rows // 2
     half = n // 2
@@ -248,7 +248,7 @@
 
     def bias_copy(k, t, owner):
         return remote(bsend, ball.at[:, pl.ds(pl.multiple_of((half if k < 2 else 0) + owner % 2 * rows, rows), rows)],
-                      bs_s, bs_r.at[k // 2], t)
+                      out_s, bs_r.at[k // 2], t)
 
     def end_bias_part(owner, i):
         return beall.at[:, pl.ds(pl.multiple_of(owner * rows + GROUP * i, GROUP), GROUP)]
@@ -256,12 +256,12 @@
     def end_bias_send(i):
         part = besend.at[:, GROUP * i:GROUP * i + GROUP]
         for k in ((0, 2), range(3))[i]:
-            remote(part, end_bias_part(sp, i), be_s, be_r.at[2 if k == 2 else i], peers[k]).start()
+            remote(part, end_bias_part(sp, i), out_s, be_r.at[2 if k == 2 else i], peers[k]).start()
 
     def end_bias_forward():
         part = end_bias_part(peers[0], 0)
         arrived(part, be_r.at[0])
-        remote(part, part, be_s, be_r.at[2], peers[2]).start()
+        remote(part, part, out_s, be_r.at[2], peers[2]).start()
 
     for k in (2, 0, 1):
         bias_copy(k, peers[k], sp).start()
@@ -315,13 +315,13 @@
         r0, size = groups[gi]
         return remote(hsend.at[0, pl.ds(t % 2 * rows + ch * cols, cols), r0:r0 + size],
                       hcol.at[pl.ds(ch * cols, cols), pl.ds(pl.multiple_of(owner * rows + r0, TILE), size)],
-                      h_s, h_r.at[ch], t)
+                      out_s, h_r.at[ch], t)
 
     def near_copy(gi, owner):
         r0, size = near[gi]
         return remote(hsend.at[1, pl.ds(pl.multiple_of((1 - core) * rows, rows), rows), r0:r0 + size],
                       hcol.at[:, pl.ds(pl.multiple_of(owner * rows + r0, TILE), size)],
-                      o_s, o_r, peers[2])
+                      out_s, o_r, peers[2])
 
     def shuffle_rows(side, r0, size):
         def body(jb, _):
@@ -396,7 +396,6 @@
     woet[...] = woe[...].T
     w1t[...] = w1[...].T
     w2t[...] = w2[...].T
-    sent(ball.at[:, 0:3 * rows], bs_s)
 
     def end_delta(p):
         hid = jnp.maximum(dot(w1t[...], u2[p % 2]), 0.0).astype(BF)
@@ -429,7 +428,7 @@
 
     def d_copy(q, count, k, t, first_col):
         return remote(dsend.at[pl.ds(2 * q, 2 * count), pl.ds(pl.multiple_of(t * rows, rows), rows)],
-                      drecv.at[pl.ds(first_col + 2 * q, 2 * count)], d_s, d_r.at[chunks if k == 2 else q // (npair // chunks)], t)
+                      drecv.at[pl.ds(first_col + 2 * q, 2 * count)], out_s, d_r.at[chunks if k == 2 else q // (npair // chunks)], t)
 
     my_cols = pl.multiple_of((2 * (1 - x) + core) * rows, rows)
 
@@ -487,10 +486,7 @@
         arrived(drecv.at[0:2 * cols], d_r.at[ch])
         for t in peers[:2]:
             final_block(0, t % 2, pl.multiple_of((2 * x + t % 2) * rows, rows), ch)
-    sent(hsend.at[0], h_s)
-    sent(ball.at[:, 0:3 * rows], be_s)
-    sent(hcol.at[:, 0:rows], o_s)
-    sent(dsend.at[:, 0:3 * rows], d_s)
+    sent(zs4.at[0:27], out_s)
 
 
 def solution(mesh):
@@ -522,7 +518,7 @@
                 vm(wqs.shape[::-1], BF), vm(wqe.shape[::-1], BF), vm(woe.shape[::-1], BF),
                 vm(w1.shape[::-1], BF), vm(w2.shape[::-1], BF),
                 vm((heads * GROUP, TILE * c), BF), vm((heads * GROUP, TILE * c), BF),
-                dma((4,)), dma((5,)), dma, dma((2,)), dma, dma((4,)), dma, dma, dma, dma((3,)), dma, dma((5,)),
+                dma((4,)), dma((5,)), dma, dma((2,)), dma((4,)), dma, dma((3,)), dma((5,)),
             ],
             compiler_params=pltpu.CompilerParams(collective_id=0, has_side_effects=True, vmem_limit_bytes=36 * 2 ** 20),
             name="pair_block",

time: 33.6 us -> 33.6 us (level)
  no operation moved by 1% of the time
where the time goes in v6:
time: 33.6 us; the launch traced here: 33.5 us
  Pallas kernels  32.1 us (96%)
  local copies, waits for them, and re-layouts  1.32 us (4%)
    pallas_call x1, Pallas kernels, local_fn(): pl.pallas_call(kernel, out_shape=vm(pair_loc.shape, F32), in_specs=[pl.Bl...  32.1 us
    unnamed x1, local copies, waits for them, and re-layouts  1.32 us

profile of v6, /device:TPU:0, one launch (start us, length us, event | category | flops | bytes accessed | tf_op | source)
XLA Modules:
  0.0 33.5 jit_solution(11770996754904600604)
XLA Ops:
  0.0 32.1 %pair_block.1 = f32[32,128,128]{2,1,0:T(8,128)S(1)} custom-call(f32[16,2,2,64,128]{4,3,2,1,0:T(8,128)} %bitcast.1, bf16[128,512]{1,0:T(8,128)(2,1)} %wqs_h.1, bf16[4,128]{1,0:T(4,128)(2,1)} %wbs_h.1, bf16[128,128]{1,0:T(8,128)(2,1)} %wos_h.1, bf16[128,512]{1,0:T(8,128)(2,1)} %wqe_h.1, bf16[4,128]{1,0:T(4,128)(2,1)} %wbe_h.1, bf16[128,128]{1,0:T(8,128)(2,1)} %woe_h.1, ...), custom_call_target="tpu_custom_call" | custom-call | tf_op jit(solution)/shard_map/pair_block/pallas_call | solution.py:504
  32.1 1.3 %copy.11 = f32[32,128,128]{2,1,0:T(8,128)} copy(f32[32,128,128]{2,1,0:T(8,128)S(1)} %pair_block.1) | data formatting | bytes 4194304
